TPU v7x, 32 devices: a whole 2x2x4 slice. The times are simulated.
32 devices in a mesh: seq: 8 (over z, y), head: 4 (over x, core).
Axes of the slice: x: 2, y: 2, z: 4, core: 2. Of those that a mesh axis runs over, the one named last changes fastest.
Arguments:
- queries: bfloat16 [1024, 12288], P('seq', 'head'), may hold values from -32 to 32
- keys: bfloat16 [1024, 768], P('seq', 'head'), may hold values from -4 to 4
- values: bfloat16 [1024, 512], P('seq', 'head'), may hold values from -6 to 6
- features: bfloat16 [1024, 2560], P('seq', 'head'), may hold values from -6 to 6
- positions: int32 [1024], P('seq'), may hold values from 0 to 767, as said below
- gate_weight: bfloat16 [2560, 128], replicated, may hold values from -0.125 to 0.125
- key_in: bfloat16 [4, 6144, 128], P('head'), may hold values from -0.078125 to 0.078125
- key_out: bfloat16 [4, 128, 192], P('head'), may hold values from -0.5 to 0.5
- value_in: bfloat16 [4, 4096, 128], P('head'), may hold values from -0.09375 to 0.09375
- value_out: bfloat16 [4, 128, 128], P('head'), may hold values from -0.5 to 0.5
Outputs:
- mixed: bfloat16 [1024, 8192], P('seq', 'head')
Inputs may be any that keep to these rules, and one draw needn't show every extreme that they name: positions rise by one from token to token and fall to 0 where one of at most three documents begins inside the slab; the first document began before or at the slab's first token and ends inside the slab.
All inputs are finite; a program needn't handle non-finite values.
Results may differ from a plain program's by a relative error of at most 0.0056.
Values may be sent and summed in bfloat16 or wider, within the bound.
No kernel may reach another device: no remote copies, remote signals or barrier semaphores. Data moves between devices by JAX's collectives and lax.ppermute only.
A program may use at most 64 MiB of HBM per device.

v0:
```python
import functools

import jax
import jax.numpy as jnp
from jax import lax
from jax.experimental import pallas as pl
from jax.experimental.pallas import tpu as pltpu
from jax.sharding import PartitionSpec as P

QH = 16
DK = 192
DV = 128
STRIDE = 16
BLOCK = 32
WINDOW = 512
LANES = 128
PAD = 256
GROUP = 4
VMEM_LIMIT = 24 << 20
MOST_SLOTS = 8

NEG = -1e30
SCALE = DK ** (-0.5) * 1.4426950408889634

f32 = jnp.float32
bf16 = jnp.bfloat16


def up(value, step):
    return -(-value // step) * step


def swap(value, axis, by):
    length = lax.axis_size(axis)
    return lax.ppermute(value, axis, [(i, i ^ by) for i in range(length)])


def turn(value, axis, by):
    length = lax.axis_size(axis)
    return lax.ppermute(value, axis, [(i, (i + by) % length) for i in range(length)])


def dot(left, right):
    return jnp.dot(left, right, preferred_element_type=f32)


def dot_t(left, right):
    return lax.dot_general(left, right, (((1,), (1,)), ((), ())), preferred_element_type=f32)


def place_hbm(value):
    return pltpu.with_memory_space_constraint(value, pltpu.HBM)


def logits_of(group, heads, features, columns, total, outs):
    total[...] = lax.dot_general(
        columns[...], features[...], (((0,), (1,)), ((), ())), preferred_element_type=f32
    )
    for step, out in enumerate(outs):
        other = group ^ step if heads & (heads - 1) == 0 else lax.rem(group + step, heads)
        out[...] = total[pl.ds(pl.multiple_of(other * (2 * QH), 2 * QH), 2 * QH), :]


def feature_copies(group, features_hbm, columns_hbm, features, columns, sems):
    depth = features.shape[1]
    first = pl.multiple_of(group * depth, LANES)
    return [
        pltpu.make_async_copy(features_hbm, features, sems.at[0]),
        pltpu.make_async_copy(columns_hbm.at[pl.ds(first, depth), :], columns, sems.at[1]),
    ]


def logit_kernel(heads, group, features_hbm, columns_hbm, *refs):
    outs, (features, columns, total, sems) = refs[:heads], refs[heads:]
    copies = feature_copies(group[0], features_hbm, columns_hbm, features, columns, sems)
    for copy in copies:
        copy.start()
    for copy in copies:
        copy.wait()
    logits_of(group[0], heads, features, columns, total, outs)


def prepare_kernel(heads, kept, offsets, codes, here_ref, group_ref, features_hbm, columns_hbm, positions_hbm, *refs):
    here, group = here_ref[0], group_ref[0]
    sources = refs[:kept]
    outs = refs[kept : kept + heads]
    bias, some, second = refs[kept + heads : kept + heads + 3]
    places = refs[kept + heads + 3 : 2 * kept + heads + 1]
    features, columns, total, positions, sems = refs[2 * kept + heads + 1 :]
    places = [*places, second.at[pl.ds(0, DK), :], second.at[pl.ds(DK, sources[-1].shape[0]), :]]
    copies = feature_copies(group, features_hbm, columns_hbm, features, columns, sems)
    copies.append(pltpu.make_async_copy(positions_hbm, positions, sems.at[2]))
    copies += [
        pltpu.make_async_copy(source, place, sems.at[3 + i])
        for i, (source, place) in enumerate(zip(sources, places))
    ]
    for copy in copies:
        copy.start()
    for copy in copies[:3]:
        copy.wait()
    logits_of(group, heads, features, columns, total, outs)
    count = positions.shape[1]
    lengths = jnp.broadcast_to(positions[...].astype(f32), (count, count)).T.astype(jnp.int32)
    token = here * count + lax.broadcasted_iota(jnp.int32, (count, count), 0)
    lane = lax.broadcasted_iota(jnp.int32, (count, count), 1)
    for step, offset in enumerate(offsets):
        key = (here - offset) * count + lane
        seen = (key <= token) & (key > token - WINDOW) & (key >= token - lengths) & (key >= 0)
        bias[:, step * count : (step + 1) * count] = jnp.where(seen, 0.0, NEG)
    near = len(offsets) * count
    most = jnp.full((count, LANES), NEG, f32)
    for start in range(near, bias.shape[1], LANES):
        code = start - near + lax.broadcasted_iota(jnp.int32, (count, LANES), 1)
        token = here * count + lax.broadcasted_iota(jnp.int32, (count, LANES), 0)
        length = lengths if count == LANES else jnp.broadcast_to(lengths[:, :1], (count, LANES))
        first = STRIDE * code
        seen = (first + (BLOCK - 1) <= token) & (first >= token - length) & (code < codes)
        part = jnp.where(seen, 0.0, NEG)
        bias[:, start : start + LANES] = part
        most = jnp.maximum(most, part)
    some[...] = jnp.where(
        jnp.broadcast_to(jnp.max(most, axis=1, keepdims=True), (count, LANES)) > 0.5 * NEG, 1.0, 0.0
    )
    for copy in copies[3:]:
        copy.wait()


def gate_shapes(count, depth, columns):
    return [
        pltpu.VMEM((count, depth), bf16),
        pltpu.VMEM((depth, columns), bf16),
        pltpu.VMEM((columns, count), f32),
    ]


def gate_logits(features, gate_weight, group, heads):
    count, depth = features.shape
    vmem, hbm = pl.BlockSpec(memory_space=pltpu.VMEM), pl.BlockSpec(memory_space=pltpu.HBM)
    return pl.pallas_call(
        functools.partial(logit_kernel, heads),
        in_specs=[pl.BlockSpec(memory_space=pltpu.SMEM), hbm, hbm],
        out_specs=[vmem] * heads,
        out_shape=[jax.ShapeDtypeStruct((2 * QH, count), f32)] * heads,
        scratch_shapes=gate_shapes(count, depth, gate_weight.shape[1])
        + [pltpu.SemaphoreType.DMA((2,))],
        compiler_params=pltpu.CompilerParams(vmem_limit_bytes=VMEM_LIMIT),
        name="gate_logits",
    )(group[None], features, gate_weight)


def prepare(here, group, positions, features, gate_weight, heads, offsets, codes, kept):
    count, depth = features.shape
    vmem, hbm = pl.BlockSpec(memory_space=pltpu.VMEM), pl.BlockSpec(memory_space=pltpu.HBM)
    wide = len(offsets) * count + up(codes, LANES)
    last = kept[-2:]
    made = pl.pallas_call(
        functools.partial(prepare_kernel, heads, len(kept), offsets, codes),
        in_specs=[pl.BlockSpec(memory_space=pltpu.SMEM)] * 2 + [hbm] * (3 + len(kept)),
        out_specs=[vmem] * (heads + 1 + len(kept)),
        out_shape=[jax.ShapeDtypeStruct((2 * QH, count), f32)] * heads
        + [
            jax.ShapeDtypeStruct((count, wide), f32),
            jax.ShapeDtypeStruct((count, LANES), f32),
            jax.ShapeDtypeStruct((last[0].shape[0] + last[1].shape[0], last[1].shape[1]), bf16),
        ]
        + [jax.ShapeDtypeStruct(value.shape, value.dtype) for value in kept[:-2]],
        scratch_shapes=gate_shapes(count, depth, gate_weight.shape[1])
        + [pltpu.VMEM((1, count), jnp.int32), pltpu.SemaphoreType.DMA((3 + len(kept),))],
        compiler_params=pltpu.CompilerParams(vmem_limit_bytes=VMEM_LIMIT),
        name="prepare",
    )(
        here[None],
        group[None],
        *[place_hbm(value) for value in (features, gate_weight, positions[None, :], *kept)],
    )
    return made[:heads], made[heads:]


def exchange(parts):
    heads = len(parts)
    if heads & (heads - 1) == 0:
        return [parts[0]] + [swap(parts[d], "head", d) for d in range(1, heads)]
    return [parts[0]] + [turn(parts[d], "head", d) for d in range(1, heads)]


def gelu(x):
    return 0.5 * x * (1.0 + jnp.tanh(0.7978845608028654 * (x + 0.044715 * x * x * x)))


def halves(rows, planes, size, weight, width):
    strides = size // STRIDE
    total = jnp.zeros((strides, 2 * LANES), f32)
    for place in range(STRIDE):
        part = jnp.concatenate(
            [rows[pl.ds(plane * size + place, strides, stride=STRIDE), :] for plane in planes], 1
        ).astype(bf16)[:, :width]
        both = jnp.concatenate(
            [
                weight[pl.ds(place * width, width), :],
                weight[pl.ds((STRIDE + place) * width, width), :],
            ],
            1,
        )
        total = total + dot(part, both)
    return total


def hidden_of(first, second):
    strides = first.shape[0]
    later = pltpu.roll(second, strides - 1, axis=0)
    last = lax.broadcasted_iota(jnp.int32, later.shape, 0) == strides - 1
    return gelu(first + jnp.where(last, 0.0, later)).astype(bf16)


def unpack(block, rows, size, at):
    count = block.shape[1]
    for plane in range(2):
        part = block[plane * LANES : min((plane + 1) * LANES, DK), :].astype(f32).T
        rows[pl.ds(plane * size + at, count), : part.shape[1]] = part
    rows[pl.ds(2 * size + at, count), :] = block[DK:, :].astype(f32)


def codes_of(rows, size, key_in, key_out, value_in, value_out):
    shares = halves(rows, (0, 1), size, key_in, DK)
    key_hidden = hidden_of(shares[:, :LANES], shares[:, LANES:])
    code_keys = dot_t(key_out[...], key_hidden).astype(bf16)
    shares = halves(rows, (2,), size, value_in, DV)
    value_hidden = hidden_of(shares[:, :LANES], shares[:, LANES:])
    code_values = dot(value_hidden, value_out[...]).astype(bf16)
    return code_keys, code_values


def attend_body(
    here, count, reach, get_block, code_keys, code_values, codes, positions, q, parts, out, scratch
):
    even, odd, near_values, far_values, near_bias, far_bias, gates = scratch
    near = (reach + 1) * count
    far = even.shape[1] - near
    lengths = jnp.broadcast_to(positions[...].astype(f32), (count, count)).T.astype(jnp.int32)

    def lens(width):
        return jnp.concatenate([lengths] * (width // count), 1) if width > count else lengths

    def ids(width, axis):
        return lax.broadcasted_iota(jnp.int32, (count, width), axis)

    token = here * count + ids(near, 0)
    key = (here - reach) * count + ids(near, 1)
    seen = (key <= token) & (key > token - WINDOW) & (key >= token - lens(near)) & (key >= 0)
    near_bias[...] = jnp.where(seen, 0.0, NEG)
    token = here * count + ids(far, 0)
    first = STRIDE * ids(far, 1)
    seen = (first + (BLOCK - 1) <= token) & (first >= token - lens(far)) & (ids(far, 1) < codes)
    far_bias[...] = jnp.where(seen, 0.0, NEG)
    some = jnp.max(jnp.where(seen, 1.0, 0.0), axis=1, keepdims=True)

    total = parts[0][...]
    for part in parts[1:]:
        total = total + part[...]
    total = jax.nn.sigmoid(total)
    total = jnp.concatenate([total, jnp.zeros((LANES - 2 * QH, count), f32)], 0).T
    coarse_lane = lax.broadcasted_iota(jnp.int32, total.shape, 1) < QH
    gates[...] = jnp.where(coarse_lane, total * some, total)

    even[DK:, :] = jnp.zeros((PAD - DK, near + far), bf16)
    odd[: PAD - DK, :] = jnp.zeros((PAD - DK, near + far), bf16)
    near_values[:, DV:] = jnp.ones((near, DV), bf16)
    far_values[:, DV:] = jnp.ones((far, DV), bf16)
    for step in range(reach + 1):
        block = get_block(jnp.maximum(here - reach + step, 0), step)
        lanes = slice(step * count, (step + 1) * count)
        even[:DK, lanes] = block[:DK, :]
        odd[PAD - DK :, lanes] = block[:DK, :]
        near_values[lanes, :DV] = block[DK:, :]
    even[:DK, near:] = code_keys
    odd[PAD - DK :, near:] = code_keys
    far_values[:, :DV] = code_values

    pair = 2 * DK
    for side in (0, 1):
        keys = (even, odd)[side]
        for chunk in range(0, QH // 2, GROUP):
            rows = jnp.concatenate(
                [
                    q[:, (chunk + j) * pair + side * LANES : (chunk + j) * pair + side * LANES + PAD]
                    for j in range(GROUP)
                ],
                0,
            )
            scores = dot(rows, keys[...])

            def branch(scores, bias, values):
                width = scores.shape[1]
                scores = scores.reshape(GROUP, count, width) + bias[...][None]
                top = jnp.max(scores, axis=2, keepdims=True)
                weights = jnp.exp2((scores - top) * SCALE).astype(bf16)
                summed = dot(weights.reshape(GROUP * count, width), values[...])
                return summed[:, :DV] / jnp.maximum(summed[:, DV:], 1.0)

            local = branch(scores[:, :near], near_bias, near_values)
            coarse = branch(scores[:, near:], far_bias, far_values)
            for j in range(GROUP):
                head = 2 * (chunk + j) + side
                at = slice(j * count, (j + 1) * count)
                mixed = (
                    gates[:, head : head + 1] * coarse[at]
                    + gates[:, QH + head : QH + head + 1] * local[at]
                )
                out[:, head * DV : (head + 1) * DV] = mixed.astype(bf16)


def attend_scratch(count, reach, far):
    near = (reach + 1) * count
    return [
        pltpu.VMEM((PAD, near + far), bf16),
        pltpu.VMEM((PAD, near + far), bf16),
        pltpu.VMEM((near, 2 * DV), bf16),
        pltpu.VMEM((far, 2 * DV), bf16),
        pltpu.VMEM((count, near), f32),
        pltpu.VMEM((count, far), f32),
        pltpu.VMEM((count, LANES), f32),
    ]


def gate_columns(parts, some):
    total = parts[0][...]
    for part in parts[1:]:
        total = total + part[...]
    total = jax.nn.sigmoid(total)
    total = jnp.concatenate([total, jnp.zeros((LANES - 2 * QH, total.shape[1]), f32)], 0).T
    coarse_lane = lax.broadcasted_iota(jnp.int32, total.shape, 1) < QH
    return jnp.where(coarse_lane, total * some, total)


def fill_keys(even, odd, lanes, keys):
    even[:DK, lanes] = keys
    even[DK:, lanes] = jnp.zeros((PAD - DK, keys.shape[1]), bf16)
    odd[: PAD - DK, lanes] = jnp.zeros((PAD - DK, keys.shape[1]), bf16)
    odd[PAD - DK :, lanes] = keys


def query_rows(q, side, chunk):
    starts = [(chunk + j) * 2 * DK + side * LANES for j in range(GROUP)]
    return jnp.concatenate([q[:, start : start + PAD] for start in starts], 0)


def place_of(here, offset):
    block = here - offset
    return jnp.where(block >= 0, (block ^ here) >> 1, 0)


def early_kernel(slots, count, offsets, here_ref, q, bias, key_in, value_in, *refs):
    blocks, (shares, summed, tops) = refs[:slots], refs[slots : slots + 3]
    held, rows, even, odd, values = refs[slots + 3 :]
    here = here_ref[0]
    for i, block in enumerate(blocks):
        held[i] = block[...]
        unpack(block, rows, slots * count, i * count)
    near = len(offsets) * count
    for step, offset in enumerate(offsets):
        block = held[place_of(here, offset)]
        lanes = slice(step * count, (step + 1) * count)
        fill_keys(even, odd, lanes, block[:DK, :])
        values[lanes, :DV] = block[DK:, :]
    values[:, DV:] = jnp.ones((near, DV), bf16)
    shares[:, : 2 * LANES] = halves(rows, (0, 1), slots * count, key_in, DK)
    shares[:, 2 * LANES :] = halves(rows, (2,), slots * count, value_in, DV)
    for side in (0, 1):
        for chunk in range(0, QH // 2, GROUP):
            scores = dot(query_rows(q, side, chunk), (even, odd)[side][...])
            scores = scores.reshape(GROUP, count, near) + bias[:, :near][None]
            top = jnp.max(scores, axis=2, keepdims=True)
            weights = jnp.exp2((scores - top) * SCALE).astype(bf16)
            at = pl.ds((side * QH // 2 + chunk) * count, GROUP * count)
            summed[at, :] = dot(weights.reshape(GROUP * count, near), values[...])
            tops[at, :] = jnp.broadcast_to(top, (GROUP, count, LANES)).reshape(GROUP * count, LANES)


def late_kernel(
    buffers, slots, heads, count, offsets, done, here_ref, q, bias, some, second, key_in, value_in, shares, summed, tops, *refs
):
    came, parts, out = refs[:buffers], refs[buffers : buffers + heads], refs[buffers + heads]
    held, rows, even, odd, values, far_values, key_shares, value_shares, gates = refs[buffers + heads + 1 :]
    size = DK + DV
    blocks = [ref.at[pl.ds(at, size), :] for ref in came for at in range(0, ref.shape[0], size)]
    here = here_ref[0]
    strides = count // STRIDE
    for i, block in enumerate(blocks):
        held[i] = block[...]
        unpack(block, rows, slots * count, i * count)
    near = len(offsets) * count
    for step, offset in enumerate(offsets):
        block = held[place_of(here, offset)]
        lanes = slice(step * count, (step + 1) * count)
        fill_keys(even, odd, lanes, block[:DK, :])
        values[lanes, :DV] = block[DK:, :]
    values[:, DV:] = jnp.ones((near, DV), bf16)
    key_late = halves(rows, (0, 1), slots * count, key_in, DK)
    value_late = halves(rows, (2,), slots * count, value_in, DV)
    for i in range(slots):
        mine = slice(i * strides, (i + 1) * strides)
        at = pl.ds(pl.multiple_of((here ^ (2 * i)) * strides, strides), strides)
        key_shares[at, :] = shares[mine, : 2 * LANES]
        value_shares[at, :] = shares[mine, 2 * LANES :]
        at = pl.ds(pl.multiple_of((here ^ (2 * i + 1)) * strides, strides), strides)
        key_shares[at, :] = key_late[mine]
        value_shares[at, :] = value_late[mine]
    codes = 2 * slots * strides
    far = far_values.shape[0]
    key_hidden = hidden_of(key_shares[:, :LANES], key_shares[:, LANES:])
    code_keys = dot_t(second[:DK, :], key_hidden).astype(bf16)
    value_hidden = hidden_of(value_shares[:, :LANES], value_shares[:, LANES:])
    code_values = dot(value_hidden, second[DK:, :]).astype(bf16)
    if far > codes:
        code_keys = jnp.concatenate([code_keys, jnp.zeros((DK, far - codes), bf16)], 1)
        code_values = jnp.concatenate([code_values, jnp.zeros((far - codes, DV), bf16)], 0)
    fill_keys(even, odd, slice(near, near + far), code_keys)
    far_values[:, :DV] = code_values
    far_values[:, DV:] = jnp.ones((far, DV), bf16)
    gates[...] = gate_columns(parts, some[...])
    size = GROUP * count
    for side in (0, 1):
        for chunk in range(0, QH // 2, GROUP):
            at = pl.ds((side * QH // 2 + chunk) * count, size)
            scores = dot(query_rows(q, side, chunk), (even, odd)[side][...])
            scores = scores.reshape(GROUP, count, near + far) + bias[:, done:][None]
            local, coarse = scores[:, :, :near], scores[:, :, near:]
            before = tops[at, :].reshape(GROUP, count, LANES)
            top = jnp.maximum(before, jnp.max(local, axis=2, keepdims=True))
            tops_near = jnp.concatenate([top] * (near // LANES), 2)
            weights = jnp.exp2((local - tops_near) * SCALE).astype(bf16)
            fade = jnp.exp2((before - top) * SCALE).reshape(size, LANES)
            old = summed[at, :] * jnp.concatenate([fade] * (2 * DV // LANES), 1)
            new = old + dot(weights.reshape(size, near), values[...])
            local = new[:, :DV] / jnp.maximum(new[:, DV:], 1.0)
            top = jnp.max(coarse, axis=2, keepdims=True)
            weights = jnp.exp2((coarse - top) * SCALE).astype(bf16)
            new = dot(weights.reshape(size, far), far_values[...])
            coarse = new[:, :DV] / jnp.maximum(new[:, DV:], 1.0)
            for j in range(GROUP):
                head = 2 * (chunk + j) + side
                mine = slice(j * count, (j + 1) * count)
                mixed = (
                    gates[:, head : head + 1] * coarse[mine]
                    + gates[:, QH + head : QH + head + 1] * local[mine]
                )
                out[:, head * DV : (head + 1) * DV] = mixed.astype(bf16)


def join_kernel(*refs):
    *blocks, out = refs
    size = blocks[0].shape[0]
    for i, block in enumerate(blocks):
        out[i * size : (i + 1) * size, :] = block[...]


def join(blocks):
    size, count = blocks[0].shape
    vmem = pl.BlockSpec(memory_space=pltpu.VMEM)
    return pl.pallas_call(
        join_kernel,
        in_specs=[vmem] * len(blocks),
        out_specs=vmem,
        out_shape=jax.ShapeDtypeStruct((len(blocks) * size, count), bf16),
        compiler_params=pltpu.CompilerParams(vmem_limit_bytes=VMEM_LIMIT),
        name="join",
    )(*blocks)


def small_slab(here, group, positions, queries, block, features, gate_weight, weights, length, heads, reach):
    count = queries.shape[0]
    codes = length * count // STRIDE
    far = up(codes, LANES)
    first = tuple(range(reach - reach % 2, -1, -2))
    then = tuple(range(reach - (reach + 1) % 2, 0, -2))
    key_in, key_out, value_in, value_out = weights
    slots = {0: block}
    for d in range(2, length, 2):
        slots[d] = swap(block, "seq", d)
    parts, (bias, some, second, queries, key_in, value_in) = prepare(
        here, group, positions, features, gate_weight, heads, first + then, codes,
        (queries, key_in, value_in, key_out, value_out),
    )
    for d in range(2, length, 2):
        slots[d] = lax.optimization_barrier((slots[d], parts))[0]
    across = [swap(block, "seq", 1)]
    across.append(swap(join([slots[d] for d in range(2, min(length, 6), 2)]), "seq", 1))
    for d in range(6, length, 2):
        across.append(swap(slots[d], "seq", 1))
    parts = exchange(parts)
    half = length // 2
    smem, vmem = pl.BlockSpec(memory_space=pltpu.SMEM), pl.BlockSpec(memory_space=pltpu.VMEM)
    params = pltpu.CompilerParams(vmem_limit_bytes=VMEM_LIMIT)
    rows = [
        pltpu.VMEM((half, DK + DV, count), bf16),
        pltpu.VMEM((3 * half * count, LANES), f32),
    ]
    near = len(first) * count
    shares, summed, tops = pl.pallas_call(
        functools.partial(early_kernel, half, count, first),
        in_specs=[smem] + [vmem] * (4 + half),
        out_specs=[vmem] * 3,
        out_shape=[
            jax.ShapeDtypeStruct((codes // 2, 4 * LANES), f32),
            jax.ShapeDtypeStruct((QH * count, 2 * DV), f32),
            jax.ShapeDtypeStruct((QH * count, LANES), f32),
        ],
        scratch_shapes=rows
        + [pltpu.VMEM((PAD, near), bf16)] * 2
        + [pltpu.VMEM((near, 2 * DV), bf16)],
        compiler_params=params,
        cost_estimate=pl.CostEstimate(flops=4 << 30, transcendentals=1 << 20, bytes_accessed=1 << 22),
        name="early",
    )(here[None], queries, bias, key_in, value_in, *[slots[d] for d in range(0, length, 2)])
    done = near
    near = len(then) * count
    return pl.pallas_call(
        functools.partial(late_kernel, len(across), half, heads, count, then, done),
        in_specs=[smem] + [vmem] * (9 + len(across) + heads),
        out_specs=vmem,
        out_shape=jax.ShapeDtypeStruct((count, QH * DV), bf16),
        scratch_shapes=rows
        + [pltpu.VMEM((PAD, near + far), bf16)] * 2
        + [pltpu.VMEM((near, 2 * DV), bf16), pltpu.VMEM((far, 2 * DV), bf16)]
        + [pltpu.VMEM((codes, 2 * LANES), f32)] * 2
        + [pltpu.VMEM((count, LANES), f32)],
        compiler_params=params,
        name="late",
    )(
        here[None], queries, bias, some, second, key_in, value_in, shares, summed, tops,
        *across, *parts,
    )


def codes_kernel(before, block, key_in, key_out, value_in, value_out, out, rows):
    count = block.shape[1]
    unpack(before[...], rows, 2 * count, 0)
    unpack(block[...], rows, 2 * count, count)
    code_keys, code_values = codes_of(rows, 2 * count, key_in, key_out, value_in, value_out)
    out[:, :DK] = code_keys.astype(f32).T
    out[:, DK:] = code_values.astype(f32)


def near_kernel(heads, count, reach, codes, here_ref, *refs):
    positions, q = refs[:2]
    blocks = refs[2 : 3 + reach]
    code_keys, code_values = refs[3 + reach : 5 + reach]
    parts = refs[5 + reach : 5 + reach + heads]
    out = refs[5 + reach + heads]
    attend_body(
        here_ref[0], count, reach, lambda at, step: blocks[step][...], code_keys[...], code_values[...],
        codes, positions, q, parts, out, refs[6 + reach + heads :],
    )


def long_slab(here, positions, queries, block, weights, parts, reach, length):
    count = queries.shape[0]
    strides = count // STRIDE
    smem, vmem = pl.BlockSpec(memory_space=pltpu.SMEM), pl.BlockSpec(memory_space=pltpu.VMEM)
    earlier = [turn(block, "seq", reach - k) for k in range(reach)]
    made = pl.pallas_call(
        codes_kernel,
        in_specs=[vmem] * 6,
        out_specs=vmem,
        out_shape=jax.ShapeDtypeStruct((2 * strides, DK + DV), f32),
        scratch_shapes=[pltpu.VMEM((6 * count, LANES), f32)],
        name="codes",
    )(earlier[-1], block, *weights)
    mine = made[strides - 1 : 2 * strides - 1].astype(bf16)
    every = lax.all_gather(mine, "seq", axis=0, tiled=True)[1:]
    codes = length * count // STRIDE
    far = up(codes, LANES)
    every = jnp.concatenate([every, jnp.zeros((far - every.shape[0], DK + DV), bf16)], 0)
    return pl.pallas_call(
        functools.partial(near_kernel, len(parts), count, reach, codes),
        in_specs=[smem] + [vmem] * (5 + reach + len(parts)),
        out_specs=vmem,
        out_shape=jax.ShapeDtypeStruct((count, QH * DV), bf16),
        scratch_shapes=attend_scratch(count, reach, far),
        name="long_slab",
    )(here[None], positions[None, :], queries, *earlier, block, every[:, :DK].T, every[:, DK:], *parts)


def on_device(
    queries, keys, values, features, positions, gate_weight, key_in, key_out, value_in, value_out
):
    count = keys.shape[0]
    length, heads = lax.axis_size("seq"), lax.axis_size("head")
    here = lax.axis_index("seq")
    group = lax.axis_index("head")
    reach = -(-WINDOW // count)
    block = jnp.concatenate([keys.T, values], 0)
    weights = (key_in[0], key_out[0].T, value_in[0], value_out[0])
    if length <= MOST_SLOTS and length > 1 and length & (length - 1) == 0:
        return small_slab(
            here, group, positions, queries, block, features, gate_weight, weights, length, heads, reach
        )
    parts = exchange(gate_logits(features, gate_weight, group, heads))
    return long_slab(here, positions, queries, block, weights, parts, reach, length)


def solution(mesh):
    return jax.shard_map(
        on_device,
        mesh=mesh,
        in_specs=(
            P("seq", "head"),
            P("seq", "head"),
            P("seq", "head"),
            P("seq", "head"),
            P("seq"),
            P(),
            P("head", None, None),
            P("head", None, None),
            P("head", None, None),
            P("head", None, None),
        ),
        out_specs=P("seq", "head"),
        check_vma=False,
    )
```

profile of v0, /device:TPU:0, one launch (start us, length us, event | category | flops | bytes accessed | tf_op | source)
XLA Modules:
  0.0 25.6 jit_solution(321447860433530001)
XLA Ops:
  0.0 0.8 %pad_maximum_fusion.refs_0_ = bf16[320,128]{1,0:T(8,128)(2,1)S(1)} fusion(bf16[128,128]{1,0:T(8,128)(2,1)} %param.12, bf16[192,128]{1,0:T(8,128)(2,1)} %bitcast.13), kind=kLoop, calls=%fused_computation | loop fusion | flops 163840 | bytes 163840 | tf_op jit(solution)/shard_map/concatenate | solution.py:592
  0.8 5.1 %collective-permute-start.2 = (bf16[320,128]{1,0:T(8,128)(2,1)S(1)}, bf16[320,128]{1,0:T(8,128)(2,1)S(1)}, u32[]{:S(2)}, u32[]{:S(2)}) collective-permute-start(bf16[320,128]{1,0:T(8,128)(2,1)S(1)} %pad_maximum_fusion.refs_0_), channel_id=1, source_target_pairs={{0,24},{4,28},{8,16},{12,20},{16,8},{20,12},{24,0},{28,4},{1,25},{... | collective-permute-start | bytes 245768 | tf_op jit(solution)/shard_map/ppermute | solution.py:35
  5.9 0.0 collective-permute-start.1
  5.9 0.6 %collective-permute-start = (bf16[320,128]{1,0:T(8,128)(2,1)S(1)}, bf16[320,128]{1,0:T(8,128)(2,1)S(1)}, u32[]{:S(2)}, u32[]{:S(2)}) collective-permute-start(bf16[320,128]{1,0:T(8,128)(2,1)S(1)} %pad_maximum_fusion.refs_0_), channel_id=1, source_target_pairs={{0,8},{4,12},{8,0},{12,4},{16,24},{20,28},{24,16},{28,20},{1,9},{5... | collective-permute-start | bytes 245768 | tf_op jit(solution)/shard_map/ppermute | solution.py:35
  6.5 2.2 %prepare.1 = (f32[32,128]{1,0:T(8,128)S(1)}, f32[32,128]{1,0:T(8,128)S(1)}, f32[32,128]{1,0:T(8,128)S(1)}, f32[32,128]{1,0:T(8,128)S(1)}, f32[128,768]{1,0:T(8,1...) custom-call(s32[1]{0:T(128)} %bitcast.here_ref, ...), custom_call_target="tpu_custom_call" | custom-call | tf_op jit(solution)/shard_map/prepare/pallas_call | solution.py:156
  8.8 0.1 collective-permute-start.6
  8.8 1.7 %collective-permute-start.3 = (bf16[320,128]{1,0:T(8,128)(2,1)S(1)}, bf16[320,128]{1,0:T(8,128)(2,1)S(1)}, u32[]{:S(2)}, u32[]{:S(2)}) collective-permute-start(bf16[320,128]{1,0:T(8,128)(2,1)S(1)} %pad_maximum_fusion.refs_0_), channel_id=1, source_target_pairs={{0,4},{4,0},{8,12},{12,8},{16,20},{20,16},{24,28},{28,24},{1,5},{5... | collective-permute-start | bytes 245768 | tf_op jit(solution)/shard_map/ppermute | solution.py:35
  10.6 0.0 collective-permute-done.2.refs_3_
  10.6 1.5 %collective-permute-start.7 = (f32[32,128]{1,0:T(8,128)S(1)}, f32[32,128]{1,0:T(8,128)S(1)}, u32[]{:S(2)}, u32[]{:S(2)}) collective-permute-start(f32[32,128]{1,0:T(8,128)S(1)} %get-tuple-element.29), channel_id=1, source_target_pairs={{0,2},{1,3},{2,0},{3,1},{4,6},{5,7},{6,4},{7,5},{8,10},{9,11},{10,... | collective-permute-start | bytes 49160 | tf_op jit(solution)/shard_map/ppermute | solution.py:35
  12.1 0.7 %collective-permute-done.1.refs_2_.refs_1_ = bf16[320,128]{1,0:T(8,128)(2,1)S(1)} collective-permute-done((bf16[320,128]{1,0:T(8,128)(2,1)S(1)}, bf16[320,128]{1,0:T(8,128)(2,1)S(1)}, u32[]{:S(2)}, u32[]{:S(2)}) %collective-permute-start.1) | collective-permute-done | bytes 81952 | tf_op jit(solution)/shard_map/ppermute | solution.py:35
  12.8 0.5 %collective-permute-start.8 = (f32[32,128]{1,0:T(8,128)S(1)}, f32[32,128]{1,0:T(8,128)S(1)}, u32[]{:S(2)}, u32[]{:S(2)}) collective-permute-start(f32[32,128]{1,0:T(8,128)S(1)} %get-tuple-element.30), channel_id=1, source_target_pairs={{0,3},{1,2},{2,1},{3,0},{4,7},{5,6},{6,5},{7,4},{8,11},{9,10},{10,... | collective-permute-start | bytes 49160 | tf_op jit(solution)/shard_map/ppermute | solution.py:35
  13.3 0.0 collective-permute-done.refs_1_.refs_0_
  13.3 1.5 %collective-permute-start.5 = (bf16[320,128]{1,0:T(8,128)(2,1)S(1)}, bf16[320,128]{1,0:T(8,128)(2,1)S(1)}, u32[]{:S(2)}, u32[]{:S(2)}) collective-permute-start(bf16[320,128]{1,0:T(8,128)(2,1)S(1)} %collective-permute-done.2.refs_3_), channel_id=1, source_target_pairs={{0,4},{4,0},{8,12},{12,8},{16,20},{20,16},{24,28},{28,24},{1,5},{5... | collective-permute-start | bytes 245768 | tf_op jit(solution)/shard_map/ppermute | solution.py:35
  14.8 0.0 collective-permute-done.6.refs_4_
  14.8 0.6 %collective-permute-start.4 = (bf16[640,128]{1,0:T(8,128)(2,1)S(1)}, bf16[640,128]{1,0:T(8,128)(2,1)S(1)}, u32[]{:S(2)}, u32[]{:S(2)}) collective-permute-start(bf16[640,128]{1,0:T(8,128)(2,1)S(1)} %join.1), channel_id=1, source_target_pairs={{0,4},{4,0},{8,12},{12,8},{16,20},{20,16},{24,28},{28,24},{1,5},{5... | collective-permute-start | bytes 491528 | tf_op jit(solution)/shard_map/ppermute | solution.py:35
  15.4 2.2 %early.1 = (f32[32,512]{1,0:T(8,128)S(1)}, f32[2048,256]{1,0:T(8,128)S(1)}, f32[2048,128]{1,0:T(8,128)S(1)}) custom-call(s32[1]{0:T(128)} %bitcast.here_ref, bf16[128,3072]{1,0:T(8,128)(2,1)S(1)} %get-tuple-element.21.q, f32[128,768]{1,0:T(8,128)S(1)} %get-tuple-element.22.bias, bf16[6144,128]{1,0:T(8,128)(2,1)S(1)} %get-tuple-element.25.key_in, ...), custom_call_target="tpu_custom_call" | custom-call | flops 4294967296 | bytes 4194304 | tf_op jit(solution)/shard_map/early/pallas_call | solution.py:499
  17.6 0.0 collective-permute-done.7.refs_5_
  17.6 0.0 collective-permute-done.8.refs_6_
  17.6 0.0 collective-permute-done.3.refs_0_
  17.6 0.8 %collective-permute-done.5.refs_2_ = bf16[320,128]{1,0:T(8,128)(2,1)S(1)} collective-permute-done((bf16[320,128]{1,0:T(8,128)(2,1)S(1)}, bf16[320,128]{1,0:T(8,128)(2,1)S(1)}, u32[]{:S(2)}, u32[]{:S(2)}) %collective-permute-start.5) | collective-permute-done | bytes 81952 | tf_op jit(solution)/shard_map/ppermute | solution.py:35
  18.4 3.5 %collective-permute-done.4.refs_1_ = bf16[640,128]{1,0:T(8,128)(2,1)S(1)} collective-permute-done((bf16[640,128]{1,0:T(8,128)(2,1)S(1)}, bf16[640,128]{1,0:T(8,128)(2,1)S(1)}, u32[]{:S(2)}, u32[]{:S(2)}) %collective-permute-start.4) | collective-permute-done | bytes 163872 | tf_op jit(solution)/shard_map/ppermute | solution.py:35
  22.0 3.6 %late.1 = bf16[128,2048]{1,0:T(8,128)(2,1)} custom-call(s32[1]{0:T(128)} %bitcast.here_ref, bf16[128,3072]{1,0:T(8,128)(2,1)S(1)} %get-tuple-element.21.q, f32[128,768]{1,0:T(8,128)S(1)} %get-tuple-element.22.bias, f32[128,128]{1,0:T(8,128)S(1)} %get-tuple-element.23.some, bf16[320,128]{1,0:T(8,128)(2,1)S(1)} %get-tuple-element.24.second, ...), custom_call_target="tpu_custom_call" | custom-call | tf_op jit(solution)/shard_map/late/pallas_call | solution.py:517
  (1 shorter events, 0.0 us)
Async XLA Ops:
  0.8 9.8 %collective-permute-start.2 = (bf16[320,128]{1,0:T(8,128)(2,1)S(1)}, bf16[320,128]{1,0:T(8,128)(2,1)S(1)}, u32[]{:S(2)}, u32[]{:S(2)}) collective-permute-start(bf16[320,128]{1,0:T(8,128)(2,1)S(1)} %pad_maximum_fusion.refs_0_), channel_id=1, source_target_pairs={{0,24},{4,28},{8,16},{12,20},{16,8},{20,12},{24,0},{28,4},{1,25},{... | collective-permute-start | bytes 245768 | tf_op jit(solution)/shard_map/ppermute | solution.py:35
  5.9 6.9 %collective-permute-start.1 = (bf16[320,128]{1,0:T(8,128)(2,1)S(1)}, bf16[320,128]{1,0:T(8,128)(2,1)S(1)}, u32[]{:S(2)}, u32[]{:S(2)}) collective-permute-start(bf16[320,128]{1,0:T(8,128)(2,1)S(1)} %pad_maximum_fusion.refs_0_), channel_id=1, source_target_pairs={{0,16},{4,20},{8,24},{12,28},{16,0},{20,4},{24,8},{28,12},{1,17},{... | collective-permute-start | bytes 245768 | tf_op jit(solution)/shard_map/ppermute | solution.py:35
  5.9 7.4 %collective-permute-start = (bf16[320,128]{1,0:T(8,128)(2,1)S(1)}, bf16[320,128]{1,0:T(8,128)(2,1)S(1)}, u32[]{:S(2)}, u32[]{:S(2)}) collective-permute-start(bf16[320,128]{1,0:T(8,128)(2,1)S(1)} %pad_maximum_fusion.refs_0_), channel_id=1, source_target_pairs={{0,8},{4,12},{8,0},{12,4},{16,24},{20,28},{24,16},{28,20},{1,9},{5... | collective-permute-start | bytes 245768 | tf_op jit(solution)/shard_map/ppermute | solution.py:35
  8.8 6.0 %collective-permute-start.6 = (f32[32,128]{1,0:T(8,128)S(1)}, f32[32,128]{1,0:T(8,128)S(1)}, u32[]{:S(2)}, u32[]{:S(2)}) collective-permute-start(f32[32,128]{1,0:T(8,128)S(1)} %get-tuple-element.28), channel_id=1, source_target_pairs={{0,1},{1,0},{2,3},{3,2},{4,5},{5,4},{6,7},{7,6},{8,9},{9,8},{10,11... | collective-permute-start | bytes 49160 | tf_op jit(solution)/shard_map/ppermute | solution.py:35
  8.8 8.8 %collective-permute-start.3 = (bf16[320,128]{1,0:T(8,128)(2,1)S(1)}, bf16[320,128]{1,0:T(8,128)(2,1)S(1)}, u32[]{:S(2)}, u32[]{:S(2)}) collective-permute-start(bf16[320,128]{1,0:T(8,128)(2,1)S(1)} %pad_maximum_fusion.refs_0_), channel_id=1, source_target_pairs={{0,4},{4,0},{8,12},{12,8},{16,20},{20,16},{24,28},{28,24},{1,5},{5... | collective-permute-start | bytes 245768 | tf_op jit(solution)/shard_map/ppermute | solution.py:35
  10.6 7.0 %collective-permute-start.7 = (f32[32,128]{1,0:T(8,128)S(1)}, f32[32,128]{1,0:T(8,128)S(1)}, u32[]{:S(2)}, u32[]{:S(2)}) collective-permute-start(f32[32,128]{1,0:T(8,128)S(1)} %get-tuple-element.29), channel_id=1, source_target_pairs={{0,2},{1,3},{2,0},{3,1},{4,6},{5,7},{6,4},{7,5},{8,10},{9,11},{10,... | collective-permute-start | bytes 49160 | tf_op jit(solution)/shard_map/ppermute | solution.py:35
  12.8 4.9 %collective-permute-start.8 = (f32[32,128]{1,0:T(8,128)S(1)}, f32[32,128]{1,0:T(8,128)S(1)}, u32[]{:S(2)}, u32[]{:S(2)}) collective-permute-start(f32[32,128]{1,0:T(8,128)S(1)} %get-tuple-element.30), channel_id=1, source_target_pairs={{0,3},{1,2},{2,1},{3,0},{4,7},{5,6},{6,5},{7,4},{8,11},{9,10},{10,... | collective-permute-start | bytes 49160 | tf_op jit(solution)/shard_map/ppermute | solution.py:35
  13.3 5.2 %collective-permute-start.5 = (bf16[320,128]{1,0:T(8,128)(2,1)S(1)}, bf16[320,128]{1,0:T(8,128)(2,1)S(1)}, u32[]{:S(2)}, u32[]{:S(2)}) collective-permute-start(bf16[320,128]{1,0:T(8,128)(2,1)S(1)} %collective-permute-done.2.refs_3_), channel_id=1, source_target_pairs={{0,4},{4,0},{8,12},{12,8},{16,20},{20,16},{24,28},{28,24},{1,5},{5... | collective-permute-start | bytes 245768 | tf_op jit(solution)/shard_map/ppermute | solution.py:35
  14.8 7.1 %collective-permute-start.4 = (bf16[640,128]{1,0:T(8,128)(2,1)S(1)}, bf16[640,128]{1,0:T(8,128)(2,1)S(1)}, u32[]{:S(2)}, u32[]{:S(2)}) collective-permute-start(bf16[640,128]{1,0:T(8,128)(2,1)S(1)} %join.1), channel_id=1, source_target_pairs={{0,4},{4,0},{8,12},{12,8},{16,20},{20,16},{24,28},{28,24},{1,5},{5... | collective-permute-start | bytes 491528 | tf_op jit(solution)/shard_map/ppermute | solution.py:35
where the time goes:
time: 25.8 us; the launch traced here: 25.6 us
  starting transfers between devices  11.6 us (45%)
  Pallas kernels  8.08 us (31%)
  waiting for transfers between devices  5.03 us (19%)
  other arithmetic  0.82 us (3%)
    ppermute x9, starting transfers between devices, swap(): return lax.ppermute(value, axis, [(i, i ^ by) for i in range(length)])  11.6 us
    ppermute x9, waiting for transfers between devices, swap(): return lax.ppermute(value, axis, [(i, i ^ by) for i in range(length)])  5.03 us
    pallas_call x1, Pallas kernels, small_slab(): pl.pallas_call(functools.partial(late_kernel, len(across), half, heads, c...  3.63 us
    pallas_call x1, Pallas kernels, small_slab(): pl.pallas_call(functools.partial(early_kernel, half, count, first), in_sp...  2.23 us
    pallas_call x1, Pallas kernels, prepare(): pl.pallas_call(functools.partial(prepare_kernel, heads, len(kept), offset...  2.21 us
    concatenate x1, other arithmetic, on_device(): block = jnp.concatenate([keys.T, values], 0)  0.82 us
  transfers between devices with their start and end apart: 9, of which 3 were waited for; matrix products, arithmetic and copies ran while one was open for 0% of the time, Pallas kernels for 17%

commit v1 on v0

--- a/solution.py
+++ b/solution.py
@@ -16,6 +16,8 @@
 LANES = 128
 PAD = 256
 GROUP = 4
+LATE_GROUP = 8
+MID_BLOCKS = 3
 VMEM_LIMIT = 24 << 20
 MOST_SLOTS = 8
 
@@ -339,8 +341,8 @@
     odd[PAD - DK :, lanes] = keys
 
 
-def query_rows(q, side, chunk):
-    starts = [(chunk + j) * 2 * DK + side * LANES for j in range(GROUP)]
+def query_rows(q, side, chunk, heads):
+    starts = [(chunk + j) * 2 * DK + side * LANES for j in range(heads)]
     return jnp.concatenate([q[:, start : start + PAD] for start in starts], 0)
 
 
@@ -367,7 +369,7 @@
     shares[:, 2 * LANES :] = halves(rows, (2,), slots * count, value_in, DV)
     for side in (0, 1):
         for chunk in range(0, QH // 2, GROUP):
-            scores = dot(query_rows(q, side, chunk), (even, odd)[side][...])
+            scores = dot(query_rows(q, side, chunk, GROUP), (even, odd)[side][...])
             scores = scores.reshape(GROUP, count, near) + bias[:, :near][None]
             top = jnp.max(scores, axis=2, keepdims=True)
             weights = jnp.exp2((scores - top) * SCALE).astype(bf16)
@@ -376,18 +378,60 @@
             tops[at, :] = jnp.broadcast_to(top, (GROUP, count, LANES)).reshape(GROUP * count, LANES)
 
 
+def split(refs):
+    size = DK + DV
+    return [ref.at[pl.ds(at, size), :] for ref in refs for at in range(0, ref.shape[0], size)]
+
+
+def codes_from(key_shares, value_shares, second, far):
+    key_hidden = hidden_of(key_shares[:, :LANES], key_shares[:, LANES:])
+    keys = dot_t(second[:DK, :], key_hidden).astype(bf16)
+    value_hidden = hidden_of(value_shares[:, :LANES], value_shares[:, LANES:])
+    values = dot(value_hidden, second[DK:, :]).astype(bf16)
+    codes = values.shape[0]
+    if far > codes:
+        keys = jnp.concatenate([keys, jnp.zeros((DK, far - codes), bf16)], 1)
+        values = jnp.concatenate([values, jnp.zeros((far - codes, DV), bf16)], 0)
+    return keys, values
+
+
+def share_rows(here, slot, strides):
+    return pl.ds(pl.multiple_of((here ^ slot) * strides, strides), strides)
+
+
+def mid_kernel(buffers, slots, count, here_ref, second, key_in, value_in, shares, *refs):
+    blocks = split(refs[:buffers])
+    key_shares, value_shares, code_keys, code_values, rows = refs[buffers:]
+    here = here_ref[0]
+    strides = count // STRIDE
+    total = len(blocks) * count
+    for i, block in enumerate(blocks):
+        unpack(block, rows, total, i * count)
+    key_mid = halves(rows, (0, 1), total, key_in, DK)
+    value_mid = halves(rows, (2,), total, value_in, DV)
+    for i in range(slots):
+        mine = slice(i * strides, (i + 1) * strides)
+        at = share_rows(here, 2 * i, strides)
+        key_shares[at, :] = shares[mine, : 2 * LANES]
+        value_shares[at, :] = shares[mine, 2 * LANES :]
+        at = share_rows(here, 2 * i + 1, strides)
+        known = i < len(blocks)
+        key_shares[at, :] = key_mid[mine] if known else jnp.zeros((strides, 2 * LANES), f32)
+        value_shares[at, :] = value_mid[mine] if known else jnp.zeros((strides, 2 * LANES), f32)
+    code_keys[...], code_values[...] = codes_from(key_shares, value_shares, second, code_values.shape[0])
+
+
 def late_kernel(
-    buffers, slots, heads, count, offsets, done, here_ref, q, bias, some, second, key_in, value_in, shares, summed, tops, *refs
+    buffers, slots, heads, count, offsets, done, here_ref, q, bias, some, second, key_in, value_in,
+    mid_key_shares, mid_value_shares, code_keys, code_values, summed, tops, *refs
 ):
     came, parts, out = refs[:buffers], refs[buffers : buffers + heads], refs[buffers + heads]
     held, rows, even, odd, values, far_values, key_shares, value_shares, gates = refs[buffers + heads + 1 :]
-    size = DK + DV
-    blocks = [ref.at[pl.ds(at, size), :] for ref in came for at in range(0, ref.shape[0], size)]
+    blocks = split(came)
     here = here_ref[0]
     strides = count // STRIDE
     for i, block in enumerate(blocks):
         held[i] = block[...]
-        unpack(block, rows, slots * count, i * count)
     near = len(offsets) * count
     for step, offset in enumerate(offsets):
         block = held[place_of(here, offset)]
@@ -395,37 +439,44 @@
         fill_keys(even, odd, lanes, block[:DK, :])
         values[lanes, :DV] = block[DK:, :]
     values[:, DV:] = jnp.ones((near, DV), bf16)
-    key_late = halves(rows, (0, 1), slots * count, key_in, DK)
-    value_late = halves(rows, (2,), slots * count, value_in, DV)
-    for i in range(slots):
-        mine = slice(i * strides, (i + 1) * strides)
-        at = pl.ds(pl.multiple_of((here ^ (2 * i)) * strides, strides), strides)
-        key_shares[at, :] = shares[mine, : 2 * LANES]
-        value_shares[at, :] = shares[mine, 2 * LANES :]
-        at = pl.ds(pl.multiple_of((here ^ (2 * i + 1)) * strides, strides), strides)
-        key_shares[at, :] = key_late[mine]
-        value_shares[at, :] = value_late[mine]
-    codes = 2 * slots * strides
     far = far_values.shape[0]
-    key_hidden = hidden_of(key_shares[:, :LANES], key_shares[:, LANES:])
-    code_keys = dot_t(second[:DK, :], key_hidden).astype(bf16)
-    value_hidden = hidden_of(value_shares[:, :LANES], value_shares[:, LANES:])
-    code_values = dot(value_hidden, second[DK:, :]).astype(bf16)
-    if far > codes:
-        code_keys = jnp.concatenate([code_keys, jnp.zeros((DK, far - codes), bf16)], 1)
-        code_values = jnp.concatenate([code_values, jnp.zeros((far - codes, DV), bf16)], 0)
-    fill_keys(even, odd, slice(near, near + far), code_keys)
-    far_values[:, :DV] = code_values
     far_values[:, DV:] = jnp.ones((far, DV), bf16)
+
+    def put(keys, found):
+        fill_keys(even, odd, slice(near, near + far), keys)
+        far_values[:, :DV] = found
+
+    last = [i for i in range(slots) if i >= MID_BLOCKS]
+    needed = functools.reduce(jnp.logical_or, [(here ^ (2 * i + 1)) < here for i in last], False)
+
+    @pl.when(needed)
+    def _():
+        total = len(last) * count
+        for j, i in enumerate(last):
+            unpack(blocks[i], rows, total, j * count)
+        key_last = halves(rows, (0, 1), total, key_in, DK)
+        value_last = halves(rows, (2,), total, value_in, DV)
+        key_shares[...] = mid_key_shares[...]
+        value_shares[...] = mid_value_shares[...]
+        for j, i in enumerate(last):
+            at = share_rows(here, 2 * i + 1, strides)
+            key_shares[at, :] = key_last[j * strides : (j + 1) * strides]
+            value_shares[at, :] = value_last[j * strides : (j + 1) * strides]
+        put(*codes_from(key_shares, value_shares, second, far))
+
+    @pl.when(jnp.logical_not(needed))
+    def _():
+        put(code_keys[...], code_values[...])
+
     gates[...] = gate_columns(parts, some[...])
-    size = GROUP * count
+    size = LATE_GROUP * count
     for side in (0, 1):
-        for chunk in range(0, QH // 2, GROUP):
+        for chunk in range(0, QH // 2, LATE_GROUP):
             at = pl.ds((side * QH // 2 + chunk) * count, size)
-            scores = dot(query_rows(q, side, chunk), (even, odd)[side][...])
-            scores = scores.reshape(GROUP, count, near + far) + bias[:, done:][None]
+            scores = dot(query_rows(q, side, chunk, LATE_GROUP), (even, odd)[side][...])
+            scores = scores.reshape(LATE_GROUP, count, near + far) + bias[:, done:][None]
             local, coarse = scores[:, :, :near], scores[:, :, near:]
-            before = tops[at, :].reshape(GROUP, count, LANES)
+            before = tops[at, :].reshape(LATE_GROUP, count, LANES)
             top = jnp.maximum(before, jnp.max(local, axis=2, keepdims=True))
             tops_near = jnp.concatenate([top] * (near // LANES), 2)
             weights = jnp.exp2((local - tops_near) * SCALE).astype(bf16)
@@ -437,7 +488,7 @@
             weights = jnp.exp2((coarse - top) * SCALE).astype(bf16)
             new = dot(weights.reshape(size, far), far_values[...])
             coarse = new[:, :DV] / jnp.maximum(new[:, DV:], 1.0)
-            for j in range(GROUP):
+            for j in range(LATE_GROUP):
                 head = 2 * (chunk + j) + side
                 mine = slice(j * count, (j + 1) * count)
                 mixed = (
@@ -514,9 +565,20 @@
     )(here[None], queries, bias, key_in, value_in, *[slots[d] for d in range(0, length, 2)])
     done = near
     near = len(then) * count
+    ahead = [value for value in across if value is not across[-1]] if len(across) > 2 else across
+    made = pl.pallas_call(
+        functools.partial(mid_kernel, len(ahead), half, count),
+        in_specs=[smem] + [vmem] * (4 + len(ahead)),
+        out_specs=[vmem] * 4,
+        out_shape=[jax.ShapeDtypeStruct((codes, 2 * LANES), f32)] * 2
+        + [jax.ShapeDtypeStruct((DK, far), bf16), jax.ShapeDtypeStruct((far, DV), bf16)],
+        scratch_shapes=[pltpu.VMEM((3 * half * count, LANES), f32)],
+        compiler_params=params,
+        name="mid",
+    )(here[None], second, key_in, value_in, shares, *ahead)
     return pl.pallas_call(
         functools.partial(late_kernel, len(across), half, heads, count, then, done),
-        in_specs=[smem] + [vmem] * (9 + len(across) + heads),
+        in_specs=[smem] + [vmem] * (12 + len(across) + heads),
         out_specs=vmem,
         out_shape=jax.ShapeDtypeStruct((count, QH * DV), bf16),
         scratch_shapes=rows
@@ -527,7 +589,7 @@
         compiler_params=params,
         name="late",
     )(
-        here[None], queries, bias, some, second, key_in, value_in, shares, summed, tops,
+        here[None], queries, bias, some, second, key_in, value_in, *made, summed, tops,
         *across, *parts,
     )
 

time: 25.8 us -> 26.2 us (1.016)
  Pallas kernels: 8.08 us -> 8.48 us
    pallas_call x0 -> x1, Pallas kernels: none -> 0.86 us  [small_slab(): pl.pallas_call(functools.partial(mid_kernel, len(ahead), half, count), in...]
    pallas_call x1, Pallas kernels: 3.63 us -> 3.17 us  [small_slab(): pl.pallas_call(functools.partial(late_kernel, len(across), half, heads, c...]
  transfers between devices with their start and end apart: 9 -> 9, of which waited for: 3 -> 2; matrix products, arithmetic and copies ran while one was open for 0% -> 0% of each run, Pallas kernels for 17% -> 20%
where the time goes in v1:
time: 26.2 us; the launch traced here: 26 us
  starting transfers between devices  11.6 us (44%)
  Pallas kernels  8.48 us (32%)
  waiting for transfers between devices  5.06 us (19%)
  other arithmetic  0.82 us (3%)
    ppermute x9, starting transfers between devices, swap(): return lax.ppermute(value, axis, [(i, i ^ by) for i in range(length)])  11.6 us
    ppermute x9, waiting for transfers between devices, swap(): return lax.ppermute(value, axis, [(i, i ^ by) for i in range(length)])  5.06 us
    pallas_call x1, Pallas kernels, small_slab(): pl.pallas_call(functools.partial(late_kernel, len(across), half, heads, c...  3.17 us
    pallas_call x1, Pallas kernels, small_slab(): pl.pallas_call(functools.partial(early_kernel, half, count, first), in_sp...  2.23 us
    pallas_call x1, Pallas kernels, prepare(): pl.pallas_call(functools.partial(prepare_kernel, heads, len(kept), offset...  2.21 us
    pallas_call x1, Pallas kernels, small_slab(): pl.pallas_call(functools.partial(mid_kernel, len(ahead), half, count), in...  0.86 us
    concatenate x1, other arithmetic, on_device(): block = jnp.concatenate([keys.T, values], 0)  0.82 us
  transfers between devices with their start and end apart: 9, of which 2 were waited for; matrix products, arithmetic and copies ran while one was open for 0% of the time, Pallas kernels for 20%

profile of v1, /device:TPU:0, one launch (start us, length us, event | category | flops | bytes accessed | tf_op | source)
XLA Modules:
  0.0 26.0 jit_solution(7043877654603092553)
XLA Ops:
  0.0 0.8 %pad_maximum_fusion.refs_0_ = bf16[320,128]{1,0:T(8,128)(2,1)S(1)} fusion(bf16[128,128]{1,0:T(8,128)(2,1)} %param.12, bf16[192,128]{1,0:T(8,128)(2,1)} %bitcast.13), kind=kLoop, calls=%fused_computation | loop fusion | flops 163840 | bytes 163840 | tf_op jit(solution)/shard_map/concatenate | solution.py:654
  0.8 5.1 %collective-permute-start.2 = (bf16[320,128]{1,0:T(8,128)(2,1)S(1)}, bf16[320,128]{1,0:T(8,128)(2,1)S(1)}, u32[]{:S(2)}, u32[]{:S(2)}) collective-permute-start(bf16[320,128]{1,0:T(8,128)(2,1)S(1)} %pad_maximum_fusion.refs_0_), channel_id=1, source_target_pairs={{0,24},{4,28},{8,16},{12,20},{16,8},{20,12},{24,0},{28,4},{1,25},{... | collective-permute-start | bytes 245768 | tf_op jit(solution)/shard_map/ppermute | solution.py:37
  5.9 0.0 collective-permute-start.1
  5.9 0.6 %collective-permute-start = (bf16[320,128]{1,0:T(8,128)(2,1)S(1)}, bf16[320,128]{1,0:T(8,128)(2,1)S(1)}, u32[]{:S(2)}, u32[]{:S(2)}) collective-permute-start(bf16[320,128]{1,0:T(8,128)(2,1)S(1)} %pad_maximum_fusion.refs_0_), channel_id=1, source_target_pairs={{0,8},{4,12},{8,0},{12,4},{16,24},{20,28},{24,16},{28,20},{1,9},{5... | collective-permute-start | bytes 245768 | tf_op jit(solution)/shard_map/ppermute | solution.py:37
  6.5 1.7 %collective-permute-start.3 = (bf16[320,128]{1,0:T(8,128)(2,1)S(1)}, bf16[320,128]{1,0:T(8,128)(2,1)S(1)}, u32[]{:S(2)}, u32[]{:S(2)}) collective-permute-start(bf16[320,128]{1,0:T(8,128)(2,1)S(1)} %pad_maximum_fusion.refs_0_), channel_id=1, source_target_pairs={{0,4},{4,0},{8,12},{12,8},{16,20},{20,16},{24,28},{28,24},{1,5},{5... | collective-permute-start | bytes 245768 | tf_op jit(solution)/shard_map/ppermute | solution.py:37
  8.2 2.2 %prepare.1 = (f32[32,128]{1,0:T(8,128)S(1)}, f32[32,128]{1,0:T(8,128)S(1)}, f32[32,128]{1,0:T(8,128)S(1)}, f32[32,128]{1,0:T(8,128)S(1)}, f32[128,768]{1,0:T(8,1...) custom-call(s32[1]{0:T(128)} %bitcast.here_ref, ...), custom_call_target="tpu_custom_call" | custom-call | tf_op jit(solution)/shard_map/prepare/pallas_call | solution.py:158
  10.4 0.1 collective-permute-start.6
  10.5 0.0 collective-permute-done.2.refs_3_
  10.5 1.5 %collective-permute-start.7 = (f32[32,128]{1,0:T(8,128)S(1)}, f32[32,128]{1,0:T(8,128)S(1)}, u32[]{:S(2)}, u32[]{:S(2)}) collective-permute-start(f32[32,128]{1,0:T(8,128)S(1)} %get-tuple-element.33), channel_id=1, source_target_pairs={{0,2},{1,3},{2,0},{3,1},{4,6},{5,7},{6,4},{7,5},{8,10},{9,11},{10,... | collective-permute-start | bytes 49160 | tf_op jit(solution)/shard_map/ppermute | solution.py:37
  12.1 0.7 %collective-permute-done.1.refs_2_.refs_1_ = bf16[320,128]{1,0:T(8,128)(2,1)S(1)} collective-permute-done((bf16[320,128]{1,0:T(8,128)(2,1)S(1)}, bf16[320,128]{1,0:T(8,128)(2,1)S(1)}, u32[]{:S(2)}, u32[]{:S(2)}) %collective-permute-start.1) | collective-permute-done | bytes 81952 | tf_op jit(solution)/shard_map/ppermute | solution.py:37
  12.8 0.5 %collective-permute-start.8 = (f32[32,128]{1,0:T(8,128)S(1)}, f32[32,128]{1,0:T(8,128)S(1)}, u32[]{:S(2)}, u32[]{:S(2)}) collective-permute-start(f32[32,128]{1,0:T(8,128)S(1)} %get-tuple-element.34), channel_id=1, source_target_pairs={{0,3},{1,2},{2,1},{3,0},{4,7},{5,6},{6,5},{7,4},{8,11},{9,10},{10,... | collective-permute-start | bytes 49160 | tf_op jit(solution)/shard_map/ppermute | solution.py:37
  13.3 0.0 collective-permute-done.refs_1_.refs_0_
  13.3 1.5 %collective-permute-start.5 = (bf16[320,128]{1,0:T(8,128)(2,1)S(1)}, bf16[320,128]{1,0:T(8,128)(2,1)S(1)}, u32[]{:S(2)}, u32[]{:S(2)}) collective-permute-start(bf16[320,128]{1,0:T(8,128)(2,1)S(1)} %collective-permute-done.2.refs_3_), channel_id=1, source_target_pairs={{0,4},{4,0},{8,12},{12,8},{16,20},{20,16},{24,28},{28,24},{1,5},{5... | collective-permute-start | bytes 245768 | tf_op jit(solution)/shard_map/ppermute | solution.py:37
  14.8 0.0 collective-permute-done.3.refs_0_
  14.8 0.6 %collective-permute-start.4 = (bf16[640,128]{1,0:T(8,128)(2,1)S(1)}, bf16[640,128]{1,0:T(8,128)(2,1)S(1)}, u32[]{:S(2)}, u32[]{:S(2)}) collective-permute-start(bf16[640,128]{1,0:T(8,128)(2,1)S(1)} %join.1), channel_id=1, source_target_pairs={{0,4},{4,0},{8,12},{12,8},{16,20},{20,16},{24,28},{28,24},{1,5},{5... | collective-permute-start | bytes 491528 | tf_op jit(solution)/shard_map/ppermute | solution.py:37
  15.4 2.2 %early.1 = (f32[32,512]{1,0:T(8,128)S(1)}, f32[2048,256]{1,0:T(8,128)S(1)}, f32[2048,128]{1,0:T(8,128)S(1)}) custom-call(s32[1]{0:T(128)} %bitcast.here_ref, bf16[128,3072]{1,0:T(8,128)(2,1)S(1)} %get-tuple-element.25.q, f32[128,768]{1,0:T(8,128)S(1)} %get-tuple-element.26.bias, bf16[6144,128]{1,0:T(8,128)(2,1)S(1)} %get-tuple-element.29.key_in, ...), custom_call_target="tpu_custom_call" | custom-call | flops 4294967296 | bytes 4194304 | tf_op jit(solution)/shard_map/early/pallas_call | solution.py:550
  17.6 4.3 %collective-permute-done.4.refs_1_ = bf16[640,128]{1,0:T(8,128)(2,1)S(1)} collective-permute-done((bf16[640,128]{1,0:T(8,128)(2,1)S(1)}, bf16[640,128]{1,0:T(8,128)(2,1)S(1)}, u32[]{:S(2)}, u32[]{:S(2)}) %collective-permute-start.4) | collective-permute-done | bytes 163872 | tf_op jit(solution)/shard_map/ppermute | solution.py:37
  22.0 0.9 %mid.1 = (f32[64,256]{1,0:T(8,128)S(1)}, f32[64,256]{1,0:T(8,128)S(1)}, bf16[192,128]{1,0:T(8,128)(2,1)S(1)}, bf16[128,128]{1,0:T(8,128)(2,1)S(1)}) custom-call(s32[1]{0:T(128)} %bitcast.here_ref, bf16[320,128]{1,0:T(8,128)(2,1)S(1)} %get-tuple-element.28.second, bf16[6144,128]{1,0:T(8,128)(2,1)S(1)} %get-tuple-element.29.key_in, ...), custom_call_target="tpu_custom_call" | custom-call | tf_op jit(solution)/shard_map/mid/pallas_call | solution.py:569
  22.8 0.0 collective-permute-done.6.refs_4_
  22.8 0.0 collective-permute-done.7.refs_5_
  22.8 0.0 collective-permute-done.8.refs_6_
  22.9 0.0 collective-permute-done.5.refs_2_
  22.9 3.2 %late.1 = bf16[128,2048]{1,0:T(8,128)(2,1)} custom-call(s32[1]{0:T(128)} %bitcast.here_ref, bf16[128,3072]{1,0:T(8,128)(2,1)S(1)} %get-tuple-element.25.q, f32[128,768]{1,0:T(8,128)S(1)} %get-tuple-element.26.bias, f32[128,128]{1,0:T(8,128)S(1)} %get-tuple-element.27.some, bf16[320,128]{1,0:T(8,128)(2,1)S(1)} %get-tuple-element.28.second, ...), custom_call_target="tpu_custom_call" | custom-call | tf_op jit(solution)/shard_map/late/pallas_call | solution.py:579
  (1 shorter events, 0.0 us)
Async XLA Ops:
  0.8 9.7 %collective-permute-start.2 = (bf16[320,128]{1,0:T(8,128)(2,1)S(1)}, bf16[320,128]{1,0:T(8,128)(2,1)S(1)}, u32[]{:S(2)}, u32[]{:S(2)}) collective-permute-start(bf16[320,128]{1,0:T(8,128)(2,1)S(1)} %pad_maximum_fusion.refs_0_), channel_id=1, source_target_pairs={{0,24},{4,28},{8,16},{12,20},{16,8},{20,12},{24,0},{28,4},{1,25},{... | collective-permute-start | bytes 245768 | tf_op jit(solution)/shard_map/ppermute | solution.py:37
  5.9 6.9 %collective-permute-start.1 = (bf16[320,128]{1,0:T(8,128)(2,1)S(1)}, bf16[320,128]{1,0:T(8,128)(2,1)S(1)}, u32[]{:S(2)}, u32[]{:S(2)}) collective-permute-start(bf16[320,128]{1,0:T(8,128)(2,1)S(1)} %pad_maximum_fusion.refs_0_), channel_id=1, source_target_pairs={{0,16},{4,20},{8,24},{12,28},{16,0},{20,4},{24,8},{28,12},{1,17},{... | collective-permute-start | bytes 245768 | tf_op jit(solution)/shard_map/ppermute | solution.py:37
  5.9 7.4 %collective-permute-start = (bf16[320,128]{1,0:T(8,128)(2,1)S(1)}, bf16[320,128]{1,0:T(8,128)(2,1)S(1)}, u32[]{:S(2)}, u32[]{:S(2)}) collective-permute-start(bf16[320,128]{1,0:T(8,128)(2,1)S(1)} %pad_maximum_fusion.refs_0_), channel_id=1, source_target_pairs={{0,8},{4,12},{8,0},{12,4},{16,24},{20,28},{24,16},{28,20},{1,9},{5... | collective-permute-start | bytes 245768 | tf_op jit(solution)/shard_map/ppermute | solution.py:37
  6.5 8.3 %collective-permute-start.3 = (bf16[320,128]{1,0:T(8,128)(2,1)S(1)}, bf16[320,128]{1,0:T(8,128)(2,1)S(1)}, u32[]{:S(2)}, u32[]{:S(2)}) collective-permute-start(bf16[320,128]{1,0:T(8,128)(2,1)S(1)} %pad_maximum_fusion.refs_0_), channel_id=1, source_target_pairs={{0,4},{4,0},{8,12},{12,8},{16,20},{20,16},{24,28},{28,24},{1,5},{5... | collective-permute-start | bytes 245768 | tf_op jit(solution)/shard_map/ppermute | solution.py:37
  10.4 12.4 %collective-permute-start.6 = (f32[32,128]{1,0:T(8,128)S(1)}, f32[32,128]{1,0:T(8,128)S(1)}, u32[]{:S(2)}, u32[]{:S(2)}) collective-permute-start(f32[32,128]{1,0:T(8,128)S(1)} %get-tuple-element.32), channel_id=1, source_target_pairs={{0,1},{1,0},{2,3},{3,2},{4,5},{5,4},{6,7},{7,6},{8,9},{9,8},{10,11... | collective-permute-start | bytes 49160 | tf_op jit(solution)/shard_map/ppermute | solution.py:37
  10.5 12.3 %collective-permute-start.7 = (f32[32,128]{1,0:T(8,128)S(1)}, f32[32,128]{1,0:T(8,128)S(1)}, u32[]{:S(2)}, u32[]{:S(2)}) collective-permute-start(f32[32,128]{1,0:T(8,128)S(1)} %get-tuple-element.33), channel_id=1, source_target_pairs={{0,2},{1,3},{2,0},{3,1},{4,6},{5,7},{6,4},{7,5},{8,10},{9,11},{10,... | collective-permute-start | bytes 49160 | tf_op jit(solution)/shard_map/ppermute | solution.py:37
  12.8 10.1 %collective-permute-start.8 = (f32[32,128]{1,0:T(8,128)S(1)}, f32[32,128]{1,0:T(8,128)S(1)}, u32[]{:S(2)}, u32[]{:S(2)}) collective-permute-start(f32[32,128]{1,0:T(8,128)S(1)} %get-tuple-element.34), channel_id=1, source_target_pairs={{0,3},{1,2},{2,1},{3,0},{4,7},{5,6},{6,5},{7,4},{8,11},{9,10},{10,... | collective-permute-start | bytes 49160 | tf_op jit(solution)/shard_map/ppermute | solution.py:37
  13.3 9.6 %collective-permute-start.5 = (bf16[320,128]{1,0:T(8,128)(2,1)S(1)}, bf16[320,128]{1,0:T(8,128)(2,1)S(1)}, u32[]{:S(2)}, u32[]{:S(2)}) collective-permute-start(bf16[320,128]{1,0:T(8,128)(2,1)S(1)} %collective-permute-done.2.refs_3_), channel_id=1, source_target_pairs={{0,4},{4,0},{8,12},{12,8},{16,20},{20,16},{24,28},{28,24},{1,5},{5... | collective-permute-start | bytes 245768 | tf_op jit(solution)/shard_map/ppermute | solution.py:37
  14.8 7.1 %collective-permute-start.4 = (bf16[640,128]{1,0:T(8,128)(2,1)S(1)}, bf16[640,128]{1,0:T(8,128)(2,1)S(1)}, u32[]{:S(2)}, u32[]{:S(2)}) collective-permute-start(bf16[640,128]{1,0:T(8,128)(2,1)S(1)} %join.1), channel_id=1, source_target_pairs={{0,4},{4,0},{8,12},{12,8},{16,20},{20,16},{24,28},{28,24},{1,5},{5... | collective-permute-start | bytes 491528 | tf_op jit(solution)/shard_map/ppermute | solution.py:37

commit v2 on v1

--- a/solution.py
+++ b/solution.py
@@ -470,32 +470,37 @@
 
     gates[...] = gate_columns(parts, some[...])
     size = LATE_GROUP * count
-    for side in (0, 1):
-        for chunk in range(0, QH // 2, LATE_GROUP):
-            at = pl.ds((side * QH // 2 + chunk) * count, size)
-            scores = dot(query_rows(q, side, chunk, LATE_GROUP), (even, odd)[side][...])
-            scores = scores.reshape(LATE_GROUP, count, near + far) + bias[:, done:][None]
-            local, coarse = scores[:, :, :near], scores[:, :, near:]
-            before = tops[at, :].reshape(LATE_GROUP, count, LANES)
-            top = jnp.maximum(before, jnp.max(local, axis=2, keepdims=True))
-            tops_near = jnp.concatenate([top] * (near // LANES), 2)
-            weights = jnp.exp2((local - tops_near) * SCALE).astype(bf16)
-            fade = jnp.exp2((before - top) * SCALE).reshape(size, LANES)
-            old = summed[at, :] * jnp.concatenate([fade] * (2 * DV // LANES), 1)
-            new = old + dot(weights.reshape(size, near), values[...])
-            local = new[:, :DV] / jnp.maximum(new[:, DV:], 1.0)
-            top = jnp.max(coarse, axis=2, keepdims=True)
-            weights = jnp.exp2((coarse - top) * SCALE).astype(bf16)
-            new = dot(weights.reshape(size, far), far_values[...])
-            coarse = new[:, :DV] / jnp.maximum(new[:, DV:], 1.0)
-            for j in range(LATE_GROUP):
-                head = 2 * (chunk + j) + side
-                mine = slice(j * count, (j + 1) * count)
-                mixed = (
-                    gates[:, head : head + 1] * coarse[mine]
-                    + gates[:, QH + head : QH + head + 1] * local[mine]
-                )
-                out[:, head * DV : (head + 1) * DV] = mixed.astype(bf16)
+
+    def normal(summed):
+        return summed[:, :DV] / jnp.maximum(summed[:, DV:], 1.0)
+
+    def attend():
+        for side in (0, 1):
+            for chunk in range(0, QH // 2, LATE_GROUP):
+                at = pl.ds((side * QH // 2 + chunk) * count, size)
+                scores = dot(query_rows(q, side, chunk, LATE_GROUP), (even, odd)[side][...])
+                scores = scores.reshape(LATE_GROUP, count, near + far) + bias[:, done:][None]
+                local, coarse = scores[:, :, :near], scores[:, :, near:]
+                before = tops[at, :].reshape(LATE_GROUP, count, LANES)
+                top = jnp.maximum(before, jnp.max(local, axis=2, keepdims=True))
+                tops_near = jnp.concatenate([top] * (near // LANES), 2)
+                weights = jnp.exp2((local - tops_near) * SCALE).astype(bf16)
+                fade = jnp.exp2((before - top) * SCALE).reshape(size, LANES)
+                old = summed[at, :] * jnp.concatenate([fade] * (2 * DV // LANES), 1)
+                local = normal(old + dot(weights.reshape(size, near), values[...]))
+                top = jnp.max(coarse, axis=2, keepdims=True)
+                weights = jnp.exp2((coarse - top) * SCALE).astype(bf16)
+                coarse = normal(dot(weights.reshape(size, far), far_values[...]))
+                for j in range(LATE_GROUP):
+                    head = 2 * (chunk + j) + side
+                    at = slice(j * count, (j + 1) * count)
+                    mixed = (
+                        gates[:, head : head + 1] * coarse[at]
+                        + gates[:, QH + head : QH + head + 1] * local[at]
+                    )
+                    out[:, head * DV : (head + 1) * DV] = mixed.astype(bf16)
+
+    pl.when(here >= 0)(attend)
 
 
 def join_kernel(*refs):

time: 26.2 us -> 26 us (level)
  transfers between devices with their start and end apart: 9 -> 9, of which waited for: 2 -> 2; matrix products, arithmetic and copies ran while one was open for 0% -> 0% of each run, Pallas kernels for 20% -> 21%
where the time goes in v2:
time: 26 us; the launch traced here: 25.9 us
  starting transfers between devices  11.6 us (45%)
  Pallas kernels  8.31 us (32%)
  waiting for transfers between devices  5.06 us (19%)
  other arithmetic  0.82 us (3%)
    ppermute x9, starting transfers between devices, swap(): return lax.ppermute(value, axis, [(i, i ^ by) for i in range(length)])  11.6 us
    ppermute x9, waiting for transfers between devices, swap(): return lax.ppermute(value, axis, [(i, i ^ by) for i in range(length)])  5.06 us
    pallas_call x1, Pallas kernels, small_slab(): pl.pallas_call(functools.partial(late_kernel, len(across), half, heads, c...  2.99 us
    pallas_call x1, Pallas kernels, small_slab(): pl.pallas_call(functools.partial(early_kernel, half, count, first), in_sp...  2.23 us
    pallas_call x1, Pallas kernels, prepare(): pl.pallas_call(functools.partial(prepare_kernel, heads, len(kept), offset...  2.21 us
    pallas_call x1, Pallas kernels, small_slab(): pl.pallas_call(functools.partial(mid_kernel, len(ahead), half, count), in...  0.86 us
    concatenate x1, other arithmetic, on_device(): block = jnp.concatenate([keys.T, values], 0)  0.82 us
  transfers between devices with their start and end apart: 9, of which 2 were waited for; matrix products, arithmetic and copies ran while one was open for 0% of the time, Pallas kernels for 21%

profile of v2, /device:TPU:0, one launch (start us, length us, event | category | flops | bytes accessed | tf_op | source)
XLA Modules:
  0.0 25.9 jit_solution(1763108024908931488)
XLA Ops:
  0.0 0.8 %pad_maximum_fusion.refs_0_ = bf16[320,128]{1,0:T(8,128)(2,1)S(1)} fusion(bf16[128,128]{1,0:T(8,128)(2,1)} %param.12, bf16[192,128]{1,0:T(8,128)(2,1)} %bitcast.13), kind=kLoop, calls=%fused_computation | loop fusion | flops 163840 | bytes 163840 | tf_op jit(solution)/shard_map/concatenate | solution.py:659
  0.8 5.1 %collective-permute-start.2 = (bf16[320,128]{1,0:T(8,128)(2,1)S(1)}, bf16[320,128]{1,0:T(8,128)(2,1)S(1)}, u32[]{:S(2)}, u32[]{:S(2)}) collective-permute-start(bf16[320,128]{1,0:T(8,128)(2,1)S(1)} %pad_maximum_fusion.refs_0_), channel_id=1, source_target_pairs={{0,24},{4,28},{8,16},{12,20},{16,8},{20,12},{24,0},{28,4},{1,25},{... | collective-permute-start | bytes 245768 | tf_op jit(solution)/shard_map/ppermute | solution.py:37
  5.9 0.0 collective-permute-start.1
  5.9 0.6 %collective-permute-start = (bf16[320,128]{1,0:T(8,128)(2,1)S(1)}, bf16[320,128]{1,0:T(8,128)(2,1)S(1)}, u32[]{:S(2)}, u32[]{:S(2)}) collective-permute-start(bf16[320,128]{1,0:T(8,128)(2,1)S(1)} %pad_maximum_fusion.refs_0_), channel_id=1, source_target_pairs={{0,8},{4,12},{8,0},{12,4},{16,24},{20,28},{24,16},{28,20},{1,9},{5... | collective-permute-start | bytes 245768 | tf_op jit(solution)/shard_map/ppermute | solution.py:37
  6.5 1.7 %collective-permute-start.3 = (bf16[320,128]{1,0:T(8,128)(2,1)S(1)}, bf16[320,128]{1,0:T(8,128)(2,1)S(1)}, u32[]{:S(2)}, u32[]{:S(2)}) collective-permute-start(bf16[320,128]{1,0:T(8,128)(2,1)S(1)} %pad_maximum_fusion.refs_0_), channel_id=1, source_target_pairs={{0,4},{4,0},{8,12},{12,8},{16,20},{20,16},{24,28},{28,24},{1,5},{5... | collective-permute-start | bytes 245768 | tf_op jit(solution)/shard_map/ppermute | solution.py:37
  8.2 2.2 %prepare.1 = (f32[32,128]{1,0:T(8,128)S(1)}, f32[32,128]{1,0:T(8,128)S(1)}, f32[32,128]{1,0:T(8,128)S(1)}, f32[32,128]{1,0:T(8,128)S(1)}, f32[128,768]{1,0:T(8,1...) custom-call(s32[1]{0:T(128)} %bitcast.here_ref, ...), custom_call_target="tpu_custom_call" | custom-call | tf_op jit(solution)/shard_map/prepare/pallas_call | solution.py:158
  10.4 0.1 collective-permute-start.6
  10.5 0.0 collective-permute-done.2.refs_3_
  10.5 1.5 %collective-permute-start.7 = (f32[32,128]{1,0:T(8,128)S(1)}, f32[32,128]{1,0:T(8,128)S(1)}, u32[]{:S(2)}, u32[]{:S(2)}) collective-permute-start(f32[32,128]{1,0:T(8,128)S(1)} %get-tuple-element.33), channel_id=1, source_target_pairs={{0,2},{1,3},{2,0},{3,1},{4,6},{5,7},{6,4},{7,5},{8,10},{9,11},{10,... | collective-permute-start | bytes 49160 | tf_op jit(solution)/shard_map/ppermute | solution.py:37
  12.1 0.7 %collective-permute-done.1.refs_2_.refs_1_ = bf16[320,128]{1,0:T(8,128)(2,1)S(1)} collective-permute-done((bf16[320,128]{1,0:T(8,128)(2,1)S(1)}, bf16[320,128]{1,0:T(8,128)(2,1)S(1)}, u32[]{:S(2)}, u32[]{:S(2)}) %collective-permute-start.1) | collective-permute-done | bytes 81952 | tf_op jit(solution)/shard_map/ppermute | solution.py:37
  12.8 0.5 %collective-permute-start.8 = (f32[32,128]{1,0:T(8,128)S(1)}, f32[32,128]{1,0:T(8,128)S(1)}, u32[]{:S(2)}, u32[]{:S(2)}) collective-permute-start(f32[32,128]{1,0:T(8,128)S(1)} %get-tuple-element.34), channel_id=1, source_target_pairs={{0,3},{1,2},{2,1},{3,0},{4,7},{5,6},{6,5},{7,4},{8,11},{9,10},{10,... | collective-permute-start | bytes 49160 | tf_op jit(solution)/shard_map/ppermute | solution.py:37
  13.3 0.0 collective-permute-done.refs_1_.refs_0_
  13.3 1.5 %collective-permute-start.5 = (bf16[320,128]{1,0:T(8,128)(2,1)S(1)}, bf16[320,128]{1,0:T(8,128)(2,1)S(1)}, u32[]{:S(2)}, u32[]{:S(2)}) collective-permute-start(bf16[320,128]{1,0:T(8,128)(2,1)S(1)} %collective-permute-done.2.refs_3_), channel_id=1, source_target_pairs={{0,4},{4,0},{8,12},{12,8},{16,20},{20,16},{24,28},{28,24},{1,5},{5... | collective-permute-start | bytes 245768 | tf_op jit(solution)/shard_map/ppermute | solution.py:37
  14.8 0.0 collective-permute-done.3.refs_0_
  14.8 0.6 %collective-permute-start.4 = (bf16[640,128]{1,0:T(8,128)(2,1)S(1)}, bf16[640,128]{1,0:T(8,128)(2,1)S(1)}, u32[]{:S(2)}, u32[]{:S(2)}) collective-permute-start(bf16[640,128]{1,0:T(8,128)(2,1)S(1)} %join.1), channel_id=1, source_target_pairs={{0,4},{4,0},{8,12},{12,8},{16,20},{20,16},{24,28},{28,24},{1,5},{5... | collective-permute-start | bytes 491528 | tf_op jit(solution)/shard_map/ppermute | solution.py:37
  15.4 2.2 %early.1 = (f32[32,512]{1,0:T(8,128)S(1)}, f32[2048,256]{1,0:T(8,128)S(1)}, f32[2048,128]{1,0:T(8,128)S(1)}) custom-call(s32[1]{0:T(128)} %bitcast.here_ref, bf16[128,3072]{1,0:T(8,128)(2,1)S(1)} %get-tuple-element.25.q, f32[128,768]{1,0:T(8,128)S(1)} %get-tuple-element.26.bias, bf16[6144,128]{1,0:T(8,128)(2,1)S(1)} %get-tuple-element.29.key_in, ...), custom_call_target="tpu_custom_call" | custom-call | flops 4294967296 | bytes 4194304 | tf_op jit(solution)/shard_map/early/pallas_call | solution.py:555
  17.6 4.3 %collective-permute-done.4.refs_1_ = bf16[640,128]{1,0:T(8,128)(2,1)S(1)} collective-permute-done((bf16[640,128]{1,0:T(8,128)(2,1)S(1)}, bf16[640,128]{1,0:T(8,128)(2,1)S(1)}, u32[]{:S(2)}, u32[]{:S(2)}) %collective-permute-start.4) | collective-permute-done | bytes 163872 | tf_op jit(solution)/shard_map/ppermute | solution.py:37
  22.0 0.9 %mid.1 = (f32[64,256]{1,0:T(8,128)S(1)}, f32[64,256]{1,0:T(8,128)S(1)}, bf16[192,128]{1,0:T(8,128)(2,1)S(1)}, bf16[128,128]{1,0:T(8,128)(2,1)S(1)}) custom-call(s32[1]{0:T(128)} %bitcast.here_ref, bf16[320,128]{1,0:T(8,128)(2,1)S(1)} %get-tuple-element.28.second, bf16[6144,128]{1,0:T(8,128)(2,1)S(1)} %get-tuple-element.29.key_in, ...), custom_call_target="tpu_custom_call" | custom-call | tf_op jit(solution)/shard_map/mid/pallas_call | solution.py:574
  22.8 0.0 collective-permute-done.6.refs_4_
  22.8 0.0 collective-permute-done.7.refs_5_
  22.8 0.0 collective-permute-done.8.refs_6_
  22.9 0.0 collective-permute-done.5.refs_2_
  22.9 3.0 %late.1 = bf16[128,2048]{1,0:T(8,128)(2,1)} custom-call(s32[1]{0:T(128)} %bitcast.here_ref, bf16[128,3072]{1,0:T(8,128)(2,1)S(1)} %get-tuple-element.25.q, f32[128,768]{1,0:T(8,128)S(1)} %get-tuple-element.26.bias, f32[128,128]{1,0:T(8,128)S(1)} %get-tuple-element.27.some, bf16[320,128]{1,0:T(8,128)(2,1)S(1)} %get-tuple-element.28.second, ...), custom_call_target="tpu_custom_call" | custom-call | tf_op jit(solution)/shard_map/late/pallas_call | solution.py:584
  (1 shorter events, 0.0 us)
Async XLA Ops:
  0.8 9.7 %collective-permute-start.2 = (bf16[320,128]{1,0:T(8,128)(2,1)S(1)}, bf16[320,128]{1,0:T(8,128)(2,1)S(1)}, u32[]{:S(2)}, u32[]{:S(2)}) collective-permute-start(bf16[320,128]{1,0:T(8,128)(2,1)S(1)} %pad_maximum_fusion.refs_0_), channel_id=1, source_target_pairs={{0,24},{4,28},{8,16},{12,20},{16,8},{20,12},{24,0},{28,4},{1,25},{... | collective-permute-start | bytes 245768 | tf_op jit(solution)/shard_map/ppermute | solution.py:37
  5.9 6.9 %collective-permute-start.1 = (bf16[320,128]{1,0:T(8,128)(2,1)S(1)}, bf16[320,128]{1,0:T(8,128)(2,1)S(1)}, u32[]{:S(2)}, u32[]{:S(2)}) collective-permute-start(bf16[320,128]{1,0:T(8,128)(2,1)S(1)} %pad_maximum_fusion.refs_0_), channel_id=1, source_target_pairs={{0,16},{4,20},{8,24},{12,28},{16,0},{20,4},{24,8},{28,12},{1,17},{... | collective-permute-start | bytes 245768 | tf_op jit(solution)/shard_map/ppermute | solution.py:37
  5.9 7.4 %collective-permute-start = (bf16[320,128]{1,0:T(8,128)(2,1)S(1)}, bf16[320,128]{1,0:T(8,128)(2,1)S(1)}, u32[]{:S(2)}, u32[]{:S(2)}) collective-permute-start(bf16[320,128]{1,0:T(8,128)(2,1)S(1)} %pad_maximum_fusion.refs_0_), channel_id=1, source_target_pairs={{0,8},{4,12},{8,0},{12,4},{16,24},{20,28},{24,16},{28,20},{1,9},{5... | collective-permute-start | bytes 245768 | tf_op jit(solution)/shard_map/ppermute | solution.py:37
  6.5 8.3 %collective-permute-start.3 = (bf16[320,128]{1,0:T(8,128)(2,1)S(1)}, bf16[320,128]{1,0:T(8,128)(2,1)S(1)}, u32[]{:S(2)}, u32[]{:S(2)}) collective-permute-start(bf16[320,128]{1,0:T(8,128)(2,1)S(1)} %pad_maximum_fusion.refs_0_), channel_id=1, source_target_pairs={{0,4},{4,0},{8,12},{12,8},{16,20},{20,16},{24,28},{28,24},{1,5},{5... | collective-permute-start | bytes 245768 | tf_op jit(solution)/shard_map/ppermute | solution.py:37
  10.4 12.4 %collective-permute-start.6 = (f32[32,128]{1,0:T(8,128)S(1)}, f32[32,128]{1,0:T(8,128)S(1)}, u32[]{:S(2)}, u32[]{:S(2)}) collective-permute-start(f32[32,128]{1,0:T(8,128)S(1)} %get-tuple-element.32), channel_id=1, source_target_pairs={{0,1},{1,0},{2,3},{3,2},{4,5},{5,4},{6,7},{7,6},{8,9},{9,8},{10,11... | collective-permute-start | bytes 49160 | tf_op jit(solution)/shard_map/ppermute | solution.py:37
  10.5 12.3 %collective-permute-start.7 = (f32[32,128]{1,0:T(8,128)S(1)}, f32[32,128]{1,0:T(8,128)S(1)}, u32[]{:S(2)}, u32[]{:S(2)}) collective-permute-start(f32[32,128]{1,0:T(8,128)S(1)} %get-tuple-element.33), channel_id=1, source_target_pairs={{0,2},{1,3},{2,0},{3,1},{4,6},{5,7},{6,4},{7,5},{8,10},{9,11},{10,... | collective-permute-start | bytes 49160 | tf_op jit(solution)/shard_map/ppermute | solution.py:37
  12.8 10.1 %collective-permute-start.8 = (f32[32,128]{1,0:T(8,128)S(1)}, f32[32,128]{1,0:T(8,128)S(1)}, u32[]{:S(2)}, u32[]{:S(2)}) collective-permute-start(f32[32,128]{1,0:T(8,128)S(1)} %get-tuple-element.34), channel_id=1, source_target_pairs={{0,3},{1,2},{2,1},{3,0},{4,7},{5,6},{6,5},{7,4},{8,11},{9,10},{10,... | collective-permute-start | bytes 49160 | tf_op jit(solution)/shard_map/ppermute | solution.py:37
  13.3 9.6 %collective-permute-start.5 = (bf16[320,128]{1,0:T(8,128)(2,1)S(1)}, bf16[320,128]{1,0:T(8,128)(2,1)S(1)}, u32[]{:S(2)}, u32[]{:S(2)}) collective-permute-start(bf16[320,128]{1,0:T(8,128)(2,1)S(1)} %collective-permute-done.2.refs_3_), channel_id=1, source_target_pairs={{0,4},{4,0},{8,12},{12,8},{16,20},{20,16},{24,28},{28,24},{1,5},{5... | collective-permute-start | bytes 245768 | tf_op jit(solution)/shard_map/ppermute | solution.py:37
  14.8 7.1 %collective-permute-start.4 = (bf16[640,128]{1,0:T(8,128)(2,1)S(1)}, bf16[640,128]{1,0:T(8,128)(2,1)S(1)}, u32[]{:S(2)}, u32[]{:S(2)}) collective-permute-start(bf16[640,128]{1,0:T(8,128)(2,1)S(1)} %join.1), channel_id=1, source_target_pairs={{0,4},{4,0},{8,12},{12,8},{16,20},{20,16},{24,28},{28,24},{1,5},{5... | collective-permute-start | bytes 491528 | tf_op jit(solution)/shard_map/ppermute | solution.py:37
